TPU v7x, 32 devices: a whole 2x2x4 slice. The times are simulated.
32 devices in a mesh: row: 4 (over y, x), col: 8 (over z, core).
Axes of the slice: x: 2, y: 2, z: 4, core: 2. Of those that a mesh axis runs over, the one named last changes fastest.
Arguments:
- adjacency: int32 [8192, 256], P('row', 'col'), may hold values from -2147483648 to 2147483647, as said below
- seed_mask: int32 [8192], P('col'), may hold values 0 or 1
- source: int32 [1], replicated, may hold values from 0 to 8191
Outputs:
- levels: int32 [8192], P('col')
- parents: int32 [8192], P('col')
Inputs may be any that keep to these rules, and one draw needn't show every extreme that they name: adjacency is symmetric (edge(u, v) = edge(v, u)); it is the union of 131072 Kronecker edges whose endpoints pick one of four quadrants per bit with weights 57, 19, 19, 5 out of 100, vertex labels not permuted, so low ids carry most edges; each word is a 32-bit pattern read as a signed int32.
All inputs are finite; a program needn't handle non-finite values.
Results may differ from a plain program's by a relative error of at most 0.000001.
Values may be sent and summed in bfloat16 or wider, within the bound.
A program may use at most 64 MiB of HBM per device.

v0:
```python
import math
import jax
import jax.numpy as jnp
from jax import lax
from jax.sharding import PartitionSpec as P

LEVELS = 4
absent = 1073741824


def from_root(block, axis, source):
    block = jnp.where(lax.axis_index(axis) == source, block, jnp.zeros_like(block))
    return lax.psum(block, axis)


def unpack(words):
    shifts = jnp.arange(32, dtype=jnp.int32)
    bit_table = jnp.bitwise_and(jnp.right_shift(words[..., None], shifts), 1)
    return bit_table.reshape(words.shape[:-1] + (words.shape[-1] * 32,))


def nearest_sources(adjacency, active, first_row):
    height = adjacency.shape[0]
    width = adjacency.shape[1] * 32
    block_rows = math.gcd(height, 256)

    def sweep_block(lowest, block_id):
        offset = block_id * block_rows
        tile_words = lax.dynamic_slice_in_dim(adjacency, offset, block_rows, 0)
        marks = lax.dynamic_slice_in_dim(active, offset, block_rows, 0)

        def scan_tile(current):
            row_ids = first_row + offset + jnp.arange(block_rows, dtype=jnp.int32)
            linked = unpack(tile_words) * marks[:, None] > 0
            found = jnp.min(jnp.where(linked, row_ids[:, None], absent), axis=0)
            return jnp.minimum(current, found)

        def keep_tile(current):
            return current

        lowest = lax.cond(jnp.any(marks > 0), scan_tile, keep_tile, lowest)
        return (lowest, None)

    start_value = jnp.full((width,), absent, jnp.int32)
    lowest, unused = lax.scan(
        sweep_block, start_value, jnp.arange(height // block_rows, dtype=jnp.int32)
    )
    return lowest


def row_frontier_of(frontier):
    col_count = lax.axis_size("col")
    row_count = lax.axis_size("row")
    owner_count = col_count // row_count
    blocks = []
    for part_no in range(owner_count):
        root_col = lax.axis_index("row") * owner_count + part_no
        blocks.append(from_root(frontier, "col", root_col))
    row_payload = jnp.concatenate(blocks, axis=0)
    return row_payload


def local(adjacency, seed_mask, source):
    height = adjacency.shape[0]
    width = adjacency.shape[1] * 32
    first_row = (lax.axis_index("row") * height).astype(jnp.int32)
    first_col = (lax.axis_index("col") * width).astype(jnp.int32)
    vertex_ids = first_col + jnp.arange(width, dtype=jnp.int32)
    reached = (seed_mask > 0) | (vertex_ids == source[0])
    levels = jnp.where(reached, 0, -1).astype(jnp.int32)
    parents = jnp.where(reached, vertex_ids, -1).astype(jnp.int32)
    frontier = reached.astype(jnp.int32)
    for depth_no in range(1, LEVELS + 1):
        row_frontier = row_frontier_of(frontier)
        nearest = nearest_sources(adjacency, row_frontier, first_row)
        nearest = lax.pmin(nearest, "row")
        fresh = (nearest < absent) & (levels < 0)
        levels = jnp.where(fresh, depth_no, levels).astype(jnp.int32)
        parents = jnp.where(fresh, nearest, parents).astype(jnp.int32)
        frontier = fresh.astype(jnp.int32)
    return (levels, parents)


def solution(mesh):
    in_specs = (P("row", "col"), P("col"), P())
    out_specs = (P("col"), P("col"))
    return jax.shard_map(local, mesh=mesh, in_specs=in_specs, out_specs=out_specs, check_vma=False)
```

profile of v0, /device:TPU:0, one launch (start us, length us, event | category | flops | bytes accessed | tf_op | source)
XLA Modules:
  0.0 188.8 jit_solution(4440167789065246323)
XLA Ops:
  1.4 10.8 %all-reduce.3 = (s32[1024]{0:T(1024)S(1)}, s32[1024]{0:T(1024)S(1)}) all-reduce(s32[1024]{0:T(1024)S(1)} %convert_select_fusion.6, s32[1024]{0:T(1024)S(1)} %get-tuple-element.372), channel_id=1, replica_groups=mesh['row'=4,'col'=8] {'col'}, use_global_device_ids=true, to_apply=%region_1.2 | all-reduce | flops 2048 | bytes 16384 | tf_op jit(solution)/shard_map/psum | solution.py:13
  12.2 24.8 %while.52 = (s32[]{:T(128)}, s32[1024]{0:T(1024)S(1)}, s32[8]{0:T(128)S(1)}, s32[2048]{0:T(1024)S(1)}, s32[2048,32]{0,1:T(8,128)}, /*index=5*/s32[]{:T(128)}, s32[]{:T(128)}, s32[1]{0:T(128)}, s32[]{:T(128)}, s32[]{:T(128)}) while((s32[]{:T(128)}, s32[1024]{0:T(1024)S(1)}, s32[8]{0:T(128)S(1)}, s32[2048]{0:T(1024)S(1)}, s32[2048,32]{0,1:T(8,128)}, ...), condition=%wide.region_7.8_spmd, body=%wide.region_2.7_spmd.sunk | while | flops 1573639 | bytes 128245 | solution.py:45
  20.3 1.6 conditional.8
  20.3 0.9 constant_dynamic-slice_fusion
  29.9 1.6 conditional.8
  30.0 0.9 constant_dynamic-slice_fusion
  37.0 8.9 %pmin.28 = s32[1024]{0:T(1024)S(1)} all-reduce(s32[1024]{0:T(1024)S(1)} %get-tuple-element.274), channel_id=1, replica_groups=mesh['row'=4,'col'=8] {'row'}, use_global_device_ids=true, to_apply=%region_8.9 | all-reduce | flops 1024 | bytes 8192 | tf_op jit(solution)/shard_map/pmin | solution.py:76
  45.9 6.3 %all-reduce.2 = (s32[1024]{0:T(1024)S(1)}, s32[1024]{0:T(1024)S(1)}) all-reduce(s32[1024]{0:T(1024)S(1)} %convert_select_fusion.4, s32[1024]{0:T(1024)S(1)} %get-tuple-element.370), channel_id=1, replica_groups=mesh['row'=4,'col'=8] {'col'}, use_global_device_ids=true, to_apply=%region_10.11 | all-reduce | flops 2048 | bytes 16384 | tf_op jit(solution)/shard_map/psum | solution.py:13
  52.3 32.7 %while.53 = (s32[]{:T(128)}, s32[1024]{0:T(1024)S(1)}, s32[8]{0:T(128)S(1)}, s32[2048]{0:T(1024)S(1)}, s32[2048,32]{0,1:T(8,128)}, /*index=5*/s32[]{:T(128)}, s32[]{:T(128)}, s32[1]{0:T(128)}, s32[]{:T(128)}, s32[]{:T(128)}) while((s32[]{:T(128)}, s32[1024]{0:T(1024)S(1)}, s32[8]{0:T(128)S(1)}, s32[2048]{0:T(1024)S(1)}, ...), condition=%wide.region_16.17_spmd, body=%wide.region_11.16_spmd.sunk | while | flops 1573639 | bytes 128245 | solution.py:45
  55.0 1.6 conditional.9
  55.0 0.9 constant_dynamic-slice_fusion.1
  59.3 1.6 conditional.9
  59.3 0.9 constant_dynamic-slice_fusion.1
  63.5 1.6 conditional.9
  63.5 0.9 constant_dynamic-slice_fusion.1
  67.8 1.6 conditional.9
  67.8 0.9 constant_dynamic-slice_fusion.1
  72.1 1.6 conditional.9
  76.4 1.6 conditional.9
  80.7 1.6 conditional.9
  80.7 0.9 constant_dynamic-slice_fusion.1
  85.0 5.6 %pmin.29 = s32[1024]{0:T(1024)S(1)} all-reduce(s32[1024]{0:T(1024)S(1)} %get-tuple-element.275), channel_id=1, replica_groups=mesh['row'=4,'col'=8] {'row'}, use_global_device_ids=true, to_apply=%region_17.18 | all-reduce | flops 1024 | bytes 8192 | tf_op jit(solution)/shard_map/pmin | solution.py:76
  90.6 8.9 %all-reduce.1 = (s32[1024]{0:T(1024)S(1)}, s32[1024]{0:T(1024)S(1)}) all-reduce(s32[1024]{0:T(1024)S(1)} %convert_select_fusion.2, s32[1024]{0:T(1024)S(1)} %get-tuple-element.368), channel_id=1, replica_groups=mesh['row'=4,'col'=8] {'col'}, use_global_device_ids=true, to_apply=%region_19.20 | all-reduce | flops 2048 | bytes 16384 | tf_op jit(solution)/shard_map/psum | solution.py:13
  99.5 34.2 %while.54 = (s32[]{:T(128)}, s32[1024]{0:T(1024)S(1)}, s32[8]{0:T(128)S(1)}, s32[2048]{0:T(1024)S(1)}, s32[2048,32]{0,1:T(8,128)}, /*index=5*/s32[]{:T(128)}, s32[]{:T(128)}, s32[1]{0:T(128)}, s32[]{:T(128)}, s32[]{:T(128)}) while((s32[]{:T(128)}, s32[1024]{0:T(1024)S(1)}, s32[8]{0:T(128)S(1)}, s32[2048]{0:T(1024)S(1)}, ...), condition=%wide.region_25.26_spmd, body=%wide.region_20.25_spmd.sunk | while | flops 1573639 | bytes 128245 | solution.py:45
  102.2 1.6 conditional.10
  106.5 1.6 conditional.10
  106.5 0.9 constant_dynamic-slice_fusion.2
  110.8 1.6 conditional.10
  115.1 1.6 conditional.10
  119.3 1.6 conditional.10
  119.4 0.9 constant_dynamic-slice_fusion.2
  123.6 1.6 conditional.10
  127.9 1.6 conditional.10
  132.2 1.6 conditional.10
  133.8 8.2 %pmin.30 = s32[1024]{0:T(1024)S(1)} all-reduce(s32[1024]{0:T(1024)S(1)} %get-tuple-element.276), channel_id=1, replica_groups=mesh['row'=4,'col'=8] {'row'}, use_global_device_ids=true, to_apply=%region_26.27 | all-reduce | flops 1024 | bytes 8192 | tf_op jit(solution)/shard_map/pmin | solution.py:76
  141.9 6.4 %all-reduce = (s32[1024]{0:T(1024)S(1)}, s32[1024]{0:T(1024)S(1)}) all-reduce(s32[1024]{0:T(1024)S(1)} %convert_select_fusion, s32[1024]{0:T(1024)S(1)} %get-tuple-element.366), channel_id=1, replica_groups=mesh['row'=4,'col'=8] {'col'}, use_global_device_ids=true, to_apply=%region_28.29 | all-reduce | flops 2048 | bytes 16384 | tf_op jit(solution)/shard_map/psum | solution.py:13
  148.4 34.2 %while.55 = (s32[]{:T(128)}, s32[1024]{0:T(1024)S(1)}, s32[8]{0:T(128)S(1)}, s32[2048]{0:T(1024)S(1)}, s32[2048,32]{0,1:T(8,128)}, /*index=5*/s32[]{:T(128)}, s32[]{:T(128)}, s32[1]{0:T(128)}, s32[]{:T(128)}, s32[]{:T(128)}) while((s32[]{:T(128)}, s32[1024]{0:T(1024)S(1)}, s32[8]{0:T(128)S(1)}, s32[2048]{0:T(1024)S(1)}, ...), condition=%wide.region_34.35_spmd, body=%wide.region_29.34_spmd.sunk | while | flops 1573639 | bytes 128245 | solution.py:45
  151.0 1.6 conditional.11
  155.3 1.6 conditional.11
  155.3 0.9 constant_dynamic-slice_fusion.3
  159.6 1.6 conditional.11
  163.9 1.6 conditional.11
  168.2 1.6 conditional.11
  172.4 1.6 conditional.11
  176.7 1.6 conditional.11
  176.7 0.9 constant_dynamic-slice_fusion.3
  181.0 1.6 conditional.11
  182.6 5.6 %pmin.31 = s32[1024]{0:T(1024)S(1)} all-reduce(s32[1024]{0:T(1024)S(1)} %get-tuple-element.277), channel_id=1, replica_groups=mesh['row'=4,'col'=8] {'row'}, use_global_device_ids=true, to_apply=%region_35.36 | all-reduce | flops 1024 | bytes 8192 | tf_op jit(solution)/shard_map/pmin | solution.py:76
  (208 shorter events, 75.0 us)
Async XLA Ops:
  0.6 0.7 copy-start
where the time goes:
time: 191 us; the launch traced here: 189 us
  blocking collectives  60.7 us (32%)
  local copies, waits for them, and re-layouts  44.5 us (23%)
  loops' own time  42 us (22%)
  other arithmetic  40.1 us (21%)
    another operation x4, loops' own time, nearest_sources(): lax.scan(sweep_block, start_value, jnp.arange(height // block_rows, dtype...  41.3 us
    psum x4, blocking collectives, from_root(): return lax.psum(block, axis)  32.4 us
    pmin x4, blocking collectives, local(): nearest = lax.pmin(nearest, 'row')  28.3 us
    reduce_or x32, other arithmetic, sweep_block(): lowest = lax.cond(jnp.any(marks > 0), scan_tile, keep_tile, lowest)  23.5 us
    dynamic_slice x25, local copies, waits for them, and re-layouts, sweep_block(): tile_words = lax.dynamic_slice_in_dim(adjacency, offset, block_rows, 0)  22 us
    dynamic_slice x32, local copies, waits for them, and re-layouts, nearest_sources(): lax.scan(sweep_block, start_value, jnp.arange(height // block_rows, dtype...  20.7 us
    reduce_min x25, other arithmetic, scan_tile(): found = jnp.min(jnp.where(linked, row_ids[:, None], absent), axis=0)  15.6 us

commit v1 on v0

--- a/solution.py
+++ b/solution.py
@@ -10,7 +10,7 @@
 
 def from_root(block, axis, source):
     block = jnp.where(lax.axis_index(axis) == source, block, jnp.zeros_like(block))
-    return lax.psum(block, axis)
+    return jnp.sum(lax.all_gather(block, axis), axis=0)
 
 
 def unpack(words):

time: 191 us -> 252 us (1.32)
  blocking collectives: 60.7 us -> 142 us
  local copies, waits for them, and re-layouts: 44.5 us -> 24.8 us
    all_gather x0 -> x8, blocking collectives: none -> 114 us  [from_root(): return jnp.sum(lax.all_gather(block, axis), axis=0)]
    psum x4 -> x0, blocking collectives: 32.4 us -> none  [from_root(): return lax.psum(block, axis)]
    dynamic_slice x25, local copies, waits for them, and re-layouts: 22 us -> 2.09 us  [sweep_block(): tile_words = lax.dynamic_slice_in_dim(adjacency, offset, block_rows, 0)]
where the time goes in v1:
time: 252 us; the launch traced here: 251 us
  blocking collectives  142 us (56%)
  loops' own time  42 us (17%)
  other arithmetic  40.8 us (16%)
  local copies, waits for them, and re-layouts  24.8 us (10%)
    all_gather x8, blocking collectives, from_root(): return jnp.sum(lax.all_gather(block, axis), axis=0)  114 us
    another operation x4, loops' own time, nearest_sources(): lax.scan(sweep_block, start_value, jnp.arange(height // block_rows, dtype...  41.3 us
    pmin x4, blocking collectives, local(): nearest = lax.pmin(nearest, 'row')  27.6 us
    reduce_or x32, other arithmetic, sweep_block(): lowest = lax.cond(jnp.any(marks > 0), scan_tile, keep_tile, lowest)  23.5 us
    dynamic_slice x32, local copies, waits for them, and re-layouts, nearest_sources(): lax.scan(sweep_block, start_value, jnp.arange(height // block_rows, dtype...  20.7 us
    reduce_min x25, other arithmetic, scan_tile(): found = jnp.min(jnp.where(linked, row_ids[:, None], absent), axis=0)  15.6 us

profile of v1, /device:TPU:0, one launch (start us, length us, event | category | flops | bytes accessed | tf_op | source)
XLA Modules:
  0.0 251.1 jit_solution(10301967488449996640)
XLA Ops:
  2.0 15.8 %all-gather.1 = s32[8192]{0:T(1024)S(1)} all-gather(s32[1024]{0:T(1024)S(1)} %convert_select_fusion.6), channel_id=3, replica_groups=mesh['row'=4,'col'=8] {'col'}, dimensions={0}, use_global_device_ids=true | all-gather | bytes 36864 | tf_op jit(solution)/shard_map/all_gather | solution.py:13
  17.9 14.1 %all-gather = s32[8192]{0:T(1024)S(1)} all-gather(s32[1024]{0:T(1024)S(1)} %get-tuple-element.388), channel_id=2, replica_groups=mesh['row'=4,'col'=8] {'col'}, dimensions={0}, use_global_device_ids=true | all-gather | bytes 36864 | tf_op jit(solution)/shard_map/all_gather | solution.py:13
  32.0 23.2 %while.52 = (s32[]{:T(128)}, s32[1024]{0:T(1024)S(1)}, s32[8]{0:T(128)S(1)}, s32[2048]{0:T(1024)S(1)}, s32[2048,32]{0,1:T(8,128)S(1)}, /*index=5*/s32[]{:T(128)}, s32[]{:T(128)}, s32[1]{0:T(128)}, s32[]{:T(128)}, s32[]{:T(128)}) while((s32[]{:T(128)}, s32[1024]{0:T(1024)S(1)}, s32[8]{0:T(128)S(1)}, s32[2048]{0:T(1024)S(1)}, ...), condition=%wide.region_7.8_spmd, body=%wide.region_2.7_spmd.sunk | while | flops 1573639 | bytes 128245 | solution.py:45
  33.3 0.7 compare_reduce_fusion.8
  36.0 0.7 compare_reduce_fusion.8
  38.8 0.7 compare_reduce_fusion.8
  40.1 0.8 conditional.8
  49.0 0.8 conditional.8
  51.1 0.7 compare_reduce_fusion.8
  55.2 8.2 %pmin.28 = s32[1024]{0:T(1024)S(1)} all-reduce(s32[1024]{0:T(1024)S(1)} %get-tuple-element.274), channel_id=1, replica_groups=mesh['row'=4,'col'=8] {'row'}, use_global_device_ids=true, to_apply=%region_8.9 | all-reduce | flops 1024 | bytes 8192 | tf_op jit(solution)/shard_map/pmin | solution.py:76
  63.4 14.1 %all-gather.3 = s32[8192]{0:T(1024)S(1)} all-gather(s32[1024]{0:T(1024)S(1)} %convert_select_fusion.4), channel_id=5, replica_groups=mesh['row'=4,'col'=8] {'col'}, dimensions={0}, use_global_device_ids=true | all-gather | bytes 36864 | tf_op jit(solution)/shard_map/all_gather | solution.py:13
  77.6 14.1 %all-gather.2 = s32[8192]{0:T(1024)S(1)} all-gather(s32[1024]{0:T(1024)S(1)} %get-tuple-element.386), channel_id=4, replica_groups=mesh['row'=4,'col'=8] {'col'}, dimensions={0}, use_global_device_ids=true | all-gather | bytes 36864 | tf_op jit(solution)/shard_map/all_gather | solution.py:13
  91.7 27.1 %while.53 = (s32[]{:T(128)}, s32[1024]{0:T(1024)S(1)}, s32[8]{0:T(128)S(1)}, s32[2048]{0:T(1024)S(1)}, s32[2048,32]{0,1:T(8,128)S(1)}, /*index=5*/s32[]{:T(128)}, s32[]{:T(128)}, s32[1]{0:T(128)}, s32[]{:T(128)}, s32[]{:T(128)}) while((s32[]{:T(128)}, s32[1024]{0:T(1024)S(1)}, s32[8]{0:T(128)S(1)}, s32[2048]{0:T(1024)S(1)}, ...), condition=%wide.region_16.17_spmd, body=%wide.region_11.16_spmd.sunk | while | flops 1573639 | bytes 128245 | solution.py:45
  94.4 0.8 conditional.9
  97.9 0.8 conditional.9
  101.4 0.8 conditional.9
  104.8 0.8 conditional.9
  108.3 0.8 conditional.9
  111.8 0.8 conditional.9
  115.3 0.8 conditional.9
  117.4 0.7 compare_reduce_fusion.9
  118.8 5.6 %pmin.29 = s32[1024]{0:T(1024)S(1)} all-reduce(s32[1024]{0:T(1024)S(1)} %get-tuple-element.275), channel_id=1, replica_groups=mesh['row'=4,'col'=8] {'row'}, use_global_device_ids=true, to_apply=%region_17.18 | all-reduce | flops 1024 | bytes 8192 | tf_op jit(solution)/shard_map/pmin | solution.py:76
  124.4 14.1 %all-gather.5 = s32[8192]{0:T(1024)S(1)} all-gather(s32[1024]{0:T(1024)S(1)} %convert_select_fusion.2), channel_id=7, replica_groups=mesh['row'=4,'col'=8] {'col'}, dimensions={0}, use_global_device_ids=true | all-gather | bytes 36864 | tf_op jit(solution)/shard_map/all_gather | solution.py:13
  138.6 14.1 %all-gather.4 = s32[8192]{0:T(1024)S(1)} all-gather(s32[1024]{0:T(1024)S(1)} %get-tuple-element.384), channel_id=6, replica_groups=mesh['row'=4,'col'=8] {'col'}, dimensions={0}, use_global_device_ids=true | all-gather | bytes 36864 | tf_op jit(solution)/shard_map/all_gather | solution.py:13
  152.7 27.9 %while.54 = (s32[]{:T(128)}, s32[1024]{0:T(1024)S(1)}, s32[8]{0:T(128)S(1)}, s32[2048]{0:T(1024)S(1)}, s32[2048,32]{0,1:T(8,128)S(1)}, /*index=5*/s32[]{:T(128)}, s32[]{:T(128)}, s32[1]{0:T(128)}, s32[]{:T(128)}, s32[]{:T(128)}) while((s32[]{:T(128)}, s32[1024]{0:T(1024)S(1)}, s32[8]{0:T(128)S(1)}, s32[2048]{0:T(1024)S(1)}, ...), condition=%wide.region_25.26_spmd, body=%wide.region_20.25_spmd.sunk | while | flops 1573639 | bytes 128245 | solution.py:45
  155.4 0.8 conditional.10
  158.9 0.8 conditional.10
  162.4 0.8 conditional.10
  165.9 0.8 conditional.10
  169.3 0.8 conditional.10
  172.8 0.8 conditional.10
  176.3 0.8 conditional.10
  179.8 0.8 conditional.10
  180.6 8.2 %pmin.30 = s32[1024]{0:T(1024)S(1)} all-reduce(s32[1024]{0:T(1024)S(1)} %get-tuple-element.276), channel_id=1, replica_groups=mesh['row'=4,'col'=8] {'row'}, use_global_device_ids=true, to_apply=%region_26.27 | all-reduce | flops 1024 | bytes 8192 | tf_op jit(solution)/shard_map/pmin | solution.py:76
  188.8 14.1 %all-gather.7 = s32[8192]{0:T(1024)S(1)} all-gather(s32[1024]{0:T(1024)S(1)} %convert_select_fusion), channel_id=9, replica_groups=mesh['row'=4,'col'=8] {'col'}, dimensions={0}, use_global_device_ids=true | all-gather | bytes 36864 | tf_op jit(solution)/shard_map/all_gather | solution.py:13
  202.9 14.1 %all-gather.6 = s32[8192]{0:T(1024)S(1)} all-gather(s32[1024]{0:T(1024)S(1)} %get-tuple-element.382), channel_id=8, replica_groups=mesh['row'=4,'col'=8] {'col'}, dimensions={0}, use_global_device_ids=true | all-gather | bytes 36864 | tf_op jit(solution)/shard_map/all_gather | solution.py:13
  217.1 27.9 %while.55 = (s32[]{:T(128)}, s32[1024]{0:T(1024)S(1)}, s32[8]{0:T(128)S(1)}, s32[2048]{0:T(1024)S(1)}, s32[2048,32]{0,1:T(8,128)S(1)}, /*index=5*/s32[]{:T(128)}, s32[]{:T(128)}, s32[1]{0:T(128)}, s32[]{:T(128)}, s32[]{:T(128)}) while((s32[]{:T(128)}, s32[1024]{0:T(1024)S(1)}, s32[8]{0:T(128)S(1)}, s32[2048]{0:T(1024)S(1)}, ...), condition=%wide.region_34.35_spmd, body=%wide.region_29.34_spmd.sunk | while | flops 1573639 | bytes 128245 | solution.py:45
  219.7 0.8 conditional.11
  223.2 0.8 conditional.11
  225.3 0.7 compare_reduce_fusion.11
  226.7 0.8 conditional.11
  230.2 0.8 conditional.11
  233.7 0.8 conditional.11
  235.8 0.7 compare_reduce_fusion.11
  237.1 0.8 conditional.11
  240.6 0.8 conditional.11
  244.1 0.8 conditional.11
  244.9 5.6 %pmin.31 = s32[1024]{0:T(1024)S(1)} all-reduce(s32[1024]{0:T(1024)S(1)} %get-tuple-element.277), channel_id=1, replica_groups=mesh['row'=4,'col'=8] {'row'}, use_global_device_ids=true, to_apply=%region_35.36 | all-reduce | flops 1024 | bytes 8192 | tf_op jit(solution)/shard_map/pmin | solution.py:76
  (228 shorter events, 60.5 us)
Async XLA Ops:
  0.6 31.4 %copy-start = (s32[2048,32]{0,1:T(8,128)S(1)}, s32[2048,32]{0,1:T(8,128)}, u32[]{:S(2)}) copy-start(s32[2048,32]{0,1:T(8,128)} %param.19) | copy-start | bytes 786436
